TPU v7x, 32 devices: a whole 2x2x4 slice. The times are simulated.
32 devices in a mesh: rows: 8 (over z, y), slab: 4 (over x, core).
Axes of the slice: x: 2, y: 2, z: 4, core: 2. Of those that a mesh axis runs over, the one named last changes fastest.
Arguments:
- snapshots: bfloat16 [65536, 2048], P(('rows', 'slab')), may hold values from -60 to 60
- start_block: float32 [2048, 64], replicated, may hold values from -6 to 6
- linear_op: float32 [64, 64], replicated, may hold values from -0.75 to 0.75
- quad_op: float32 [4096, 64], replicated, may hold values from -0.009765625 to 0.009765625
- offset: float32 [64], replicated, may hold values from -3 to 3
Outputs:
- projection: bfloat16 [65536, 64], P(('rows', 'slab'))
- reduced: float32 [2048, 64], P(('rows', 'slab'))
- mismatch: float32 [2048, 64], P(('rows', 'slab'))
All inputs are finite; a program needn't handle non-finite values.
Results may differ from a plain program's by a relative error of at most 0.0029.
Values sent between devices are 32-bit elements; how exact they have to be, the bound alone decides.
A program may use at most 128 MiB of HBM per device.

v0:
```python
import math

import jax
import jax.numpy as jnp
from jax import lax
from jax.sharding import PartitionSpec as P


def shifted(block, axis, distance):
    devices = range(lax.axis_size(axis))
    route = [(i - distance, i) for i in devices if i - distance in devices]
    return lax.ppermute(block, axis, route)


def advance(state, linear_op, quad_op, offset):
    pairs = (state[:, :, None] * state[:, None, :]).reshape(state.shape[0], -1)
    highest = lax.Precision.HIGHEST
    change = (
        jnp.dot(state, linear_op, precision=highest)
        + jnp.dot(pairs, quad_op, precision=highest)
        + offset[None, :]
    )
    return state + 0.25 * change


def normalize(power):
    highest = lax.Precision.HIGHEST
    factor = jnp.linalg.cholesky(jnp.dot(power.T, power, precision=highest))
    return jax.scipy.linalg.solve_triangular(factor, power.T, lower=True).T


def body(snapshots, start_block, linear_op, quad_op, offset):
    highest = lax.Precision.HIGHEST
    devices = lax.axis_size(("rows", "slab"))
    width = snapshots.shape[1]
    share = width // devices
    total = snapshots.shape[0] * devices
    factor_scale = math.sqrt(width) / total
    contract = (((0,), (0,)), ((), ()))
    gram_block = lax.psum_scatter(
        lax.dot_general(snapshots, snapshots, contract, preferred_element_type=jnp.float32),
        ("rows", "slab"),
        scatter_dimension=0,
        tiled=True,
    )
    power_block = jnp.dot(gram_block, start_block, precision=highest)
    power = lax.all_gather(power_block, ("rows", "slab"), axis=0, tiled=True)
    basis = normalize(power)
    modes = jnp.dot(snapshots, basis, precision=highest, preferred_element_type=jnp.float32)
    projection = modes.astype(jnp.bfloat16)
    reduced = jnp.dot(gram_block, basis, precision=highest) * factor_scale
    state = advance(advance(reduced, linear_op, quad_op, offset), linear_op, quad_op, offset)
    following = shifted(reduced[:2], ("rows", "slab"), -1)
    target = jnp.concatenate([reduced[2:], following], axis=0)
    position = lax.axis_index(("rows", "slab")) * share + jnp.arange(share, dtype=jnp.int32)
    mismatch = jnp.where((position < width - 2)[:, None], state - target, jnp.float32(0.0))
    return (projection, reduced, mismatch)


def solution(mesh):
    in_specs = (P(("rows", "slab"), None), P(), P(), P(), P())
    out_specs = (P(("rows", "slab"), None), P(("rows", "slab"), None), P(("rows", "slab"), None))
    return jax.shard_map(body, mesh=mesh, in_specs=in_specs, out_specs=out_specs, check_vma=False)
```

profile of v0, /device:TPU:1, one launch (start us, length us, event | category | flops | bytes accessed | tf_op | source)
XLA Modules:
  0.0 311.9 jit_solution(9003682272394563611)
XLA Ops:
  7.2 0.0 reduce-scatter.2.cloned.1.call-start
  7.2 24.4 %fusion.12 = f32[2048,2048]{1,0:T(8,128)} fusion(bf16[2048,2048]{1,0:T(8,128)(2,1)} %param.5), kind=kOutput, calls=%fused_computation.26 | convolution fusion | flops 17179869184 | bytes 25165824 | tf_op jit(solution)/shard_map/dot_general | solution.py:41
  31.7 185.5 %reduce-scatter.2.cloned.1.call-done = f32[64,2048]{1,0:T(8,128)} async-done(((f32[2048,2048]{1,0:T(8,128)}), f32[64,2048]{1,0:T(8,128)}) %reduce-scatter.2.cloned.1.call-update) | async-done | bytes 524304 | tf_op jit(solution)/shard_map/reduce_scatter | solution.py:40
  217.2 1.6 fusion.13
  218.8 45.4 %all_gather.3 = f32[2048,64]{1,0:T(8,128)S(1)} all-gather(f32[64,64]{1,0:T(8,128)S(1)} %fusion.13), channel_id=1, replica_groups=mesh['rows'=8,'slab'=4] {'rows','slab'}, dimensions={0}, use_global_device_ids=true | all-gather | bytes 540672 | tf_op jit(solution)/shard_map/all_gather | solution.py:47
  264.2 1.9 fusion.14
  266.1 0.1 copy.8
  266.2 5.8 %cholesky.16 = f32[64,64]{1,0:T(8,128)S(1)} custom-call(f32[64,64]{1,0:T(8,128)S(1)} %fusion.11), custom_call_target="Cholesky" | custom-call | tf_op jit(solution)/shard_map/jit(cholesky)/cholesky | solution.py:28
  272.1 0.6 compare_reduce_fusion
  272.7 0.7 fusion.7
  273.4 4.9 %custom-call.7 = f32[1,64,64]{1,2,0:T(8,128)S(1)} custom-call(f32[1,64,64]{2,1,0:T(8,128)S(1)} %fusion.7), custom_call_target="InvertDiagBlocksLowerTriangular" | custom-call | tf_op jit(solution)/shard_map/jit(_solve_triangular)/triangular_solve | solution.py:29
  278.3 1.3 fusion.9
  279.6 1.6 convolution_multiply_fusion
  281.2 0.6 broadcast_multiply_fusion.1
  281.9 10.7 %fusion = bf16[2048,64]{0,1:T(8,128)(2,1)} fusion(f32[64,2048]{1,0:T(8,128)S(1)} %fusion.9, bf16[2048,2048]{1,0:T(8,128)(2,1)} %param.5), kind=kOutput, calls=%fused_computation.1 | convolution fusion | flops 3221356544 | bytes 9175040 | tf_op jit(solution)/shard_map/dot_general | solution.py:49
  292.6 1.6 mul.59
  294.3 0.2 fusion.15
  294.4 2.2 fusion.6
  296.7 0.6 broadcast_multiply_fusion
  297.3 2.1 collective-permute-start
  299.4 0.2 fusion.16
  299.6 1.6 mul.64
  301.2 1.0 collective-permute-done
  302.2 2.8 fusion.8
  (16 shorter events, 0.1 us)
Async XLA Ops:
  7.2 287.3 %copy-start = (f32[4096,64]{0,1:T(8,128)S(1)}, f32[4096,64]{0,1:T(8,128)}, u32[]{:S(2)}) copy-start(f32[4096,64]{0,1:T(8,128)} %param.8) | copy-start | bytes 3145732
  7.2 210.0 %reduce-scatter.2.cloned.1.call-start = ((), (), s32[]{:S(2)}) async-start(), calls=%async_computation.1 | async-start | bytes 17301504 | tf_op jit(solution)/shard_map/reduce_scatter | solution.py:40
  31.7 185.5 %copy-start.2 = (f32[2048,64]{0,1:T(8,128)S(1)}, f32[2048,64]{0,1:T(8,128)}, u32[]{:S(2)}) copy-start(f32[2048,64]{0,1:T(8,128)} %param.6) | copy-start | bytes 1572868
  278.3 16.0 %copy-start.3 = (f32[64,64]{1,0:T(8,128)S(1)}, f32[64,64]{1,0:T(8,128)}, u32[]{:S(2)}) copy-start(f32[64,64]{1,0:T(8,128)} %param.7) | copy-start | bytes 49156
  278.3 16.1 %copy-start.4 = (f32[64]{0:T(128)S(1)}, f32[64]{0:T(128)}, u32[]{:S(2)}) copy-start(f32[64]{0:T(128)} %param.9) | copy-start | bytes 772
  281.2 18.3 %copy-start.1 = (f32[64,64]{1,0:T(8,128)}, f32[64,64]{1,0:T(8,128)S(1)}, u32[]{:S(2)}) copy-start(f32[64,64]{1,0:T(8,128)S(1)} %convolution_multiply_fusion) | copy-start | bytes 49156
  297.3 4.9 %collective-permute-start = (f32[2,64]{1,0:T(2,128)S(1)}, f32[2,64]{1,0:T(2,128)S(1)}, u32[]{:S(2)}, u32[]{:S(2)}) collective-permute-start(f32[2,64]{1,0:T(2,128)S(1)} %slice.21), channel_id=1, source_target_pairs={{1,0},{2,1},{3,2},{4,3},{5,4},{6,5},{7,6},{8,7},{9,8},{10,9},{11,1... | collective-permute-start | bytes 1544 | tf_op jit(solution)/shard_map/ppermute | solution.py:12
Sparse Core Ops, SparseCore 0:
  31.8 185.3 reduce-scatter.1
where the time goes:
time: 312 us
  waiting for transfers between devices  186 us (60%)
  matrix products  46.9 us (15%)
  blocking collectives  45.4 us (15%)
  between operations  14.2 us (5%)
  other arithmetic  13.3 us (4%)
  local copies, waits for them, and re-layouts  3.4 us (1%)
    reduce_scatter x1, waiting for transfers between devices, body(): lax.psum_scatter(lax.dot_general(snapshots, snapshots, contract, preferre...  185 us
    all_gather x1, blocking collectives, body(): power = lax.all_gather(power_block, ('rows', 'slab'), axis=0, tiled=True)  45.4 us
    dot_general x1, matrix products, body(): lax.dot_general(snapshots, snapshots, contract, preferred_element_type=jn...  24.4 us
    dot_general x1, matrix products, body(): jnp.dot(snapshots, basis, precision=highest, preferred_element_type=jnp.f...  10.7 us
    another operation x3, other arithmetic, normalize(): factor = jnp.linalg.cholesky(jnp.dot(power.T, power, precision=highest))  6.52 us
  transfers between devices with their start and end apart: 2, of which 2 were waited for; matrix products, arithmetic and copies ran while one was open for 1% of the time, Pallas kernels for 0%

commit v1 on v0

v1 whole, which is shorter than its diff:
```python
import functools
import math

import jax
import jax.numpy as jnp
from jax import lax
from jax.experimental import pallas as pl
from jax.experimental.pallas import tpu as pltpu
from jax.sharding import PartitionSpec as P

MESH = pl.DeviceIdType.MESH
LANES = 128
SUBLANES = 8
VMEM_SPEC = pl.BlockSpec(memory_space=pltpu.VMEM)
F32 = jnp.float32
BF16 = jnp.bfloat16
HIGHEST = lax.Precision.HIGHEST


def split(x):
    high = x.astype(BF16)
    low = (x - high.astype(F32)).astype(BF16)
    return high, low


def dot(a, b, contract):
    return lax.dot_general(a, b, (contract, ((), ())), preferred_element_type=F32)


def pass_over(snap_ref, cat_ref, acc_ref):
    rank = cat_ref.shape[1] // 2
    step = pl.program_id(0)
    both = dot(snap_ref[...], cat_ref[...], ((1,), (0,)))
    y = both[:, :rank] + both[:, rank:]
    high, low = split(y)
    ycat = jnp.concatenate([high, low], axis=1)
    part = dot(ycat, snap_ref[...], ((0,), (0,)))
    folded = part[:rank] + part[rank:]

    @pl.when(step == 0)
    def _():
        acc_ref[...] = folded

    @pl.when(step > 0)
    def _():
        acc_ref[...] += folded

    return y


def power_kernel(snap_ref, start_ref, out_ref, cat_ref, acc_ref):
    @pl.when(pl.program_id(0) == 0)
    def _():
        cat_ref[...] = jnp.concatenate(split(start_ref[...]), axis=1)

    pass_over(snap_ref, cat_ref, acc_ref)

    @pl.when(pl.program_id(0) == pl.num_programs(0) - 1)
    def _():
        rank, width = acc_ref.shape
        per_row = width // LANES
        per_chunk = out_ref.shape[1] // SUBLANES
        for t in range(rank // SUBLANES * per_row):
            i, j = divmod(t, per_row)
            tile = acc_ref[i * SUBLANES : (i + 1) * SUBLANES, j * LANES : (j + 1) * LANES]
            d, r = divmod(t, per_chunk)
            out_ref[d, r * SUBLANES : (r + 1) * SUBLANES, :] = tile


def coords_kernel(snap_ref, power_ref, out_ref, w_ref, corr_ref, cat_ref, acc_ref):
    @pl.when(pl.program_id(0) == 0)
    def _():
        pt = power_ref[...]
        cat_ref[...] = jnp.concatenate(split(pt.T), axis=1)
        high, low = split(pt)
        contract = ((1,), (1,))
        corr_ref[...] = dot(high, high, contract) + (dot(high, low, contract) + dot(low, high, contract))

    w_ref[...] = pass_over(snap_ref, cat_ref, acc_ref)

    @pl.when(pl.program_id(0) == pl.num_programs(0) - 1)
    def _():
        n, rows, _ = out_ref.shape
        share = acc_ref.shape[1] // n
        groups = LANES // share
        for d in range(n):
            lo = d * share
            parts = [acc_ref[g * rows : (g + 1) * rows, lo : lo + share] for g in range(groups)]
            out_ref[d] = jnp.concatenate(parts, axis=1) if groups > 1 else parts[0]


def place(index, slab):
    return (index // slab, lax.rem(index, slab))


def everyone(n, slab, me, fn):
    def one(s, _):
        peer = lax.rem(me + s, n)
        fn(s, peer, place(peer, slab))
        return 0

    lax.fori_loop(1, n, one, 0)


def enter(n, slab, me):
    barrier = pltpu.get_barrier_semaphore()
    everyone(
        n, slab, me,
        lambda s, peer, where: pl.semaphore_signal(barrier, inc=1, device_id=where, device_id_type=MESH),
    )
    pl.semaphore_wait(barrier, n - 1)


def scatter_copy(part_ref, recv_ref, send_sem, recv_sem, s, peer, where):
    return pltpu.make_async_remote_copy(
        src_ref=part_ref.at[peer], dst_ref=recv_ref.at[s],
        send_sem=send_sem.at[s], recv_sem=recv_sem.at[s],
        device_id=where, device_id_type=MESH,
    )


def total_of(n, me, part_ref, recv_ref):
    total = part_ref[me]
    return lax.fori_loop(1, n, lambda s, t: t + recv_ref[s], total)


def reduce_kernel(n, slab, part_ref, out_ref, recv_ref, full_ref, send_sem, recv_sem, send2, recv2):
    me = lax.axis_index(("rows", "slab"))
    enter(n, slab, me)
    make = functools.partial(scatter_copy, part_ref, recv_ref, send_sem, recv_sem)
    everyone(n, slab, me, lambda *a: make(*a).start())
    everyone(n, slab, me, lambda *a: make(*a).wait_recv())
    full_ref[me] = total_of(n, me, part_ref, recv_ref)

    def spread(s, peer, where):
        return pltpu.make_async_remote_copy(
            src_ref=full_ref.at[me], dst_ref=full_ref.at[me],
            send_sem=send2.at[s], recv_sem=recv2.at[s],
            device_id=where, device_id_type=MESH,
        )

    def arrival(s, peer, where):
        source = lax.rem(me + n - s, n)
        return pltpu.make_async_remote_copy(
            src_ref=full_ref.at[source], dst_ref=full_ref.at[source],
            send_sem=send2.at[s], recv_sem=recv2.at[s],
            device_id=where, device_id_type=MESH,
        )

    everyone(n, slab, me, lambda *a: spread(*a).start())
    everyone(n, slab, me, lambda *a: arrival(*a).wait_recv())
    rank, width = out_ref.shape
    per_row = width // LANES
    per_chunk = full_ref.shape[1] // SUBLANES
    for t in range(rank // SUBLANES * per_row):
        i, j = divmod(t, per_row)
        d, r = divmod(t, per_chunk)
        tile = full_ref[d, r * SUBLANES : (r + 1) * SUBLANES, :]
        out_ref[i * SUBLANES : (i + 1) * SUBLANES, j * LANES : (j + 1) * LANES] = tile
    everyone(n, slab, me, lambda *a: make(*a).wait_send())
    everyone(n, slab, me, lambda *a: spread(*a).wait_send())


def invert_factor(corr, work_ref):
    rank = corr.shape[0]
    row = lax.broadcasted_iota(jnp.int32, (rank, rank), 0)
    col = lax.broadcasted_iota(jnp.int32, (rank, rank), 1)
    eye = jnp.where(row == col, 1.0, 0.0).astype(F32)
    work_ref[...] = jnp.concatenate([corr, eye], axis=1)
    rows1 = lax.broadcasted_iota(jnp.int32, (rank, 1), 0)
    lanes = lax.broadcasted_iota(jnp.int32, (rank, 2 * rank), 1)
    lane1 = lax.broadcasted_iota(jnp.int32, (1, 2 * rank), 1)

    def eliminate(j, _):
        m = work_ref[...]
        pivot = work_ref[pl.ds(j, 1), :]
        column = jnp.sum(jnp.where(lanes == j, m, 0.0), axis=1, keepdims=True)
        d = jnp.sum(jnp.where(lane1 == j, pivot, 0.0), axis=1, keepdims=True)
        factor = jnp.where(rows1 > j, column / d, 0.0)
        work_ref[...] = m - factor * pivot
        return 0

    lax.fori_loop(0, rank, eliminate, 0)
    m = work_ref[...]
    diag = jnp.sum(jnp.where(row == col, m[:, :rank], 0.0), axis=1, keepdims=True)
    return m[:, rank:] / jnp.sqrt(diag)


def finish_kernel(n, slab, scale, part_ref, corr_ref, w_ref, lin_ref, quad_ref, off_ref,
                  proj_ref, red_ref, mis_ref,
                  recv_ref, work_ref, qcat_ref, edge_ref, halo_ref, send_sem, recv_sem, edge_send, edge_recv):
    me = lax.axis_index(("rows", "slab"))
    enter(n, slab, me)
    make = functools.partial(scatter_copy, part_ref, recv_ref, send_sem, recv_sem)
    everyone(n, slab, me, lambda *a: make(*a).start())

    inverse = invert_factor(corr_ref[...], work_ref)
    ihigh, ilow = split(inverse)
    nt = ((1,), (1,))
    block = min(w_ref.shape[0], 512)

    def modes_of(b, _):
        rows = pl.ds(pl.multiple_of(b * block, block), block)
        whigh, wlow = split(w_ref[rows, :])
        modes = dot(whigh, ihigh, nt) + (dot(whigh, ilow, nt) + dot(wlow, ihigh, nt))
        proj_ref[rows, :] = modes.astype(BF16)
        return 0

    lax.fori_loop(0, w_ref.shape[0] // block, modes_of, 0)
    rank = inverse.shape[0]
    qt = quad_ref[...].T
    qhigh, qlow = split(qt)
    qcat_ref[:rank, :] = qhigh
    qcat_ref[rank:, :] = qlow
    lin_t = lin_ref[...].T
    off_t = off_ref[...].T

    everyone(n, slab, me, lambda *a: make(*a).wait_recv())
    total = total_of(n, me, part_ref, recv_ref)
    share = red_ref.shape[0]
    groups = LANES // share
    if groups > 1:
        total = jnp.concatenate([total[:, g * share : (g + 1) * share] for g in range(groups)], axis=0)
    z = jnp.dot(inverse, total, precision=HIGHEST, preferred_element_type=F32) * scale
    reduced = z.T
    red_ref[...] = reduced
    edge_ref[...] = reduced[:SUBLANES]

    before = place(lax.rem(me + n - 1, n), slab)
    edge = pltpu.make_async_remote_copy(
        src_ref=edge_ref, dst_ref=halo_ref, send_sem=edge_send, recv_sem=edge_recv,
        device_id=before, device_id_type=MESH,
    )
    edge.start()

    state = z
    for _ in range(2):
        pairs = (state[:, None, :] * state[None, :, :]).reshape(rank * rank, share)
        phigh, plow = split(pairs)
        nn = ((1,), (0,))
        both = dot(qcat_ref[...], phigh, nn)
        quad = both[:rank] + (both[rank:] + dot(qcat_ref[:rank, :], plow, nn))
        change = jnp.dot(lin_t, state, precision=HIGHEST, preferred_element_type=F32) + quad + off_t
        state = state + 0.25 * change
    rolled = state.T
    edge.wait_recv()
    target = jnp.concatenate([reduced[2:], halo_ref[...][:2]], axis=0)
    position = me * share + lax.broadcasted_iota(jnp.int32, (share, 1), 0)
    mis_ref[...] = jnp.where(position < n * share - 2, rolled - target, 0.0)
    edge.wait_send()
    everyone(n, slab, me, lambda *a: make(*a).wait_send())


def body(snapshots, start_block, linear_op, quad_op, offset, *, n, slab):
    rows, width = snapshots.shape
    rank = start_block.shape[1]
    share = width // n
    tiles = rank * width // n // LANES
    scale = math.sqrt(width) / (rows * n)
    block = min(rows, 512)
    snap_spec = pl.BlockSpec((block, width), lambda i: (i, 0))
    whole = lambda shape: pl.BlockSpec(shape, lambda i: (0,) * len(shape))
    scratch = [pltpu.VMEM((width, 2 * rank), BF16), pltpu.VMEM((rank, width), F32)]
    arbitrary = pltpu.CompilerParams(dimension_semantics=("arbitrary",), vmem_limit_bytes=56 * 2**20)
    cost = pl.CostEstimate(flops=8 * rows * width * rank, bytes_accessed=rows * width * 2, transcendentals=0)
    part = pl.pallas_call(
        power_kernel,
        grid=(rows // block,),
        in_specs=[snap_spec, whole((width, rank))],
        out_specs=whole((n, tiles, LANES)),
        out_shape=jax.ShapeDtypeStruct((n, tiles, LANES), F32),
        scratch_shapes=scratch, compiler_params=arbitrary, cost_estimate=cost, name="power",
    )(snapshots, start_block)

    sems = lambda: pltpu.SemaphoreType.DMA((n,))
    power_t = pl.pallas_call(
        functools.partial(reduce_kernel, n, slab),
        in_specs=[VMEM_SPEC],
        out_specs=VMEM_SPEC,
        out_shape=jax.ShapeDtypeStruct((rank, width), F32),
        scratch_shapes=[pltpu.VMEM((n, tiles, LANES), F32), pltpu.VMEM((n, tiles, LANES), F32), sems(), sems(), sems(), sems()],
        compiler_params=pltpu.CompilerParams(collective_id=0, has_side_effects=True),
        name="allreduce",
    )(part)

    zpart, w, corr = pl.pallas_call(
        coords_kernel,
        grid=(rows // block,),
        in_specs=[snap_spec, whole((rank, width))],
        out_specs=[whole((n, tiles, LANES)), pl.BlockSpec((block, rank), lambda i: (i, 0)), whole((rank, rank))],
        out_shape=[
            jax.ShapeDtypeStruct((n, tiles, LANES), F32),
            jax.ShapeDtypeStruct((rows, rank), F32),
            jax.ShapeDtypeStruct((rank, rank), F32),
        ],
        scratch_shapes=scratch, compiler_params=arbitrary, cost_estimate=cost, name="coords",
    )(snapshots, power_t)

    return pl.pallas_call(
        functools.partial(finish_kernel, n, slab, scale),
        in_specs=[VMEM_SPEC] * 6,
        out_specs=[VMEM_SPEC] * 3,
        out_shape=[
            jax.ShapeDtypeStruct((rows, rank), BF16),
            jax.ShapeDtypeStruct((share, rank), F32),
            jax.ShapeDtypeStruct((share, rank), F32),
        ],
        scratch_shapes=[
            pltpu.VMEM((n, tiles, LANES), F32),
            pltpu.VMEM((rank, 2 * rank), F32),
            pltpu.VMEM((2 * rank, rank * rank), BF16),
            pltpu.VMEM((SUBLANES, rank), F32),
            pltpu.VMEM((SUBLANES, rank), F32),
            sems(), sems(), pltpu.SemaphoreType.DMA, pltpu.SemaphoreType.DMA,
        ],
        compiler_params=pltpu.CompilerParams(collective_id=1, has_side_effects=True, vmem_limit_bytes=56 * 2**20),
        name="finish",
    )(zpart, corr, w, linear_op, quad_op, offset.reshape(1, rank))


def solution(mesh):
    in_specs = (P(("rows", "slab"), None), P(), P(), P(), P())
    out_specs = (P(("rows", "slab"), None), P(("rows", "slab"), None), P(("rows", "slab"), None))
    slab = mesh.shape["slab"]
    run = functools.partial(body, n=mesh.shape["rows"] * slab, slab=slab)
    return jax.shard_map(run, mesh=mesh, in_specs=in_specs, out_specs=out_specs, check_vma=False)
```

time: 312 us -> 89 us (0.29)
  the two profiles are of different devices: /device:TPU:1 before, /device:TPU:13 now
where the time goes in v1:
time: 89 us; the launch traced here: 88.6 us
  Pallas kernels  78.9 us (89%)
  local copies, waits for them, and re-layouts  8.99 us (10%)
    pallas_call x1, Pallas kernels, body(): pl.pallas_call(functools.partial(reduce_kernel, n, slab), in_specs=[VMEM_...  31.9 us
    pallas_call x1, Pallas kernels, body(): pl.pallas_call(functools.partial(finish_kernel, n, slab, scale), in_specs...  26.1 us
    pallas_call x1, Pallas kernels, body(): pl.pallas_call(coords_kernel, grid=(rows // block,), in_specs=[snap_spec,...  10.7 us
    pallas_call x1, Pallas kernels, body(): pl.pallas_call(power_kernel, grid=(rows // block,), in_specs=[snap_spec,...  10.3 us
    unnamed x6, local copies, waits for them, and re-layouts  7.05 us
    pallas_call x1, local copies, waits for them, and re-layouts, body(): pl.pallas_call(functools.partial(finish_kernel, n, slab, scale), in_specs...  1.93 us

profile of v1, /device:TPU:13, one launch (start us, length us, event | category | flops | bytes accessed | tf_op | source)
XLA Modules:
  0.0 88.6 jit_solution(9259880685087097065)
XLA Ops:
  0.6 2.4 %copy.8.start_ref = f32[2048,64]{1,0:T(8,128)} copy(f32[2048,64]{0,1:T(8,128)} %param.6) | data formatting | bytes 1048576 | tf_op args[1]
  3.0 0.0 copy-start
  3.0 10.3 %power.1.part_ref = f32[32,32,128]{2,1,0:T(8,128)} custom-call(bf16[2048,2048]{1,0:T(8,128)(2,1)} %snap_ref.3, f32[2048,64]{1,0:T(8,128)} %copy.8.start_ref), custom_call_target="tpu_custom_call" | custom-call | flops 2147483648 | bytes 8388608 | tf_op jit(solution)/shard_map/power/pallas_call | solution.py:266
  13.3 31.9 %allreduce.1.power_ref = f32[64,2048]{1,0:T(8,128)} custom-call(f32[32,32,128]{2,1,0:T(8,128)} %power.1.part_ref), custom_call_target="tpu_custom_call" | custom-call | tf_op jit(solution)/shard_map/allreduce/pallas_call | solution.py:276
  45.1 10.7 %coords.1 = (f32[32,32,128]{2,1,0:T(8,128)}, f32[2048,64]{1,0:T(8,128)}, f32[64,64]{1,0:T(8,128)}) custom-call(bf16[2048,2048]{1,0:T(8,128)(2,1)} %snap_ref.3, f32[64,2048]{1,0:T(8,128)} %allreduce.1.power_ref), custom_call_target="tpu_custom_call" | custom-call | flops 2147483648 | bytes 8388608 | tf_op jit(solution)/shard_map/coords/pallas_call | solution.py:286
  55.8 0.0 copy-done
  55.8 1.9 %copy.9.quad_ref = f32[4096,64]{1,0:T(8,128)} copy(f32[4096,64]{0,1:T(8,128)S(1)} %copy-done) | data formatting | bytes 2097152 | tf_op args[3]
  57.8 26.1 %finish.1 = (bf16[2048,64]{1,0:T(8,128)(2,1)}, f32[64,64]{1,0:T(8,128)}, f32[64,64]{1,0:T(8,128)}) custom-call(f32[32,32,128]{2,1,0:T(8,128)} %get-tuple-element.6.part_ref, f32[64,64]{1,0:T(8,128)} %get-tuple-element.7.corr_ref, f32[2048,64]{1,0:T(8,128)} %get-tuple-element.8.w_ref, f32[64,64]{1,0:T(8,128)} %lin_ref.1, f32[4096,64]{1,0:T(8,128)} %copy.9.quad_ref, ...), custom_call_target="tpu_custom_call" | custom-call | tf_op jit(solution)/shard_map/finish/pallas_call | solution.py:299
  83.9 1.9 %copy.10 = bf16[2048,64]{0,1:T(8,128)(2,1)} copy(bf16[2048,64]{1,0:T(8,128)(2,1)} %get-tuple-element.9) | data formatting | bytes 524288 | tf_op jit(solution)/shard_map/finish/pallas_call | solution.py:299
  85.8 1.4 %copy.13 = f32[64,64]{1,0:T(8,128)} copy(f32[64,64]{1,0:T(8,128)} %get-tuple-element.16) | data formatting | bytes 32768
  87.2 1.4 %copy.14 = f32[64,64]{1,0:T(8,128)} copy(f32[64,64]{1,0:T(8,128)} %get-tuple-element.17) | data formatting | bytes 32768
Async XLA Ops:
  3.0 52.8 %copy-start = (f32[4096,64]{0,1:T(8,128)S(1)}, f32[4096,64]{0,1:T(8,128)}, u32[]{:S(2)}) copy-start(f32[4096,64]{0,1:T(8,128)} %param.8) | copy-start | bytes 3145732

commit v2 on v0

v2 whole, which is shorter than its diff:
```python
import functools
import math

import jax
import jax.numpy as jnp
from jax import lax
from jax.experimental import pallas as pl
from jax.experimental.pallas import tpu as pltpu
from jax.sharding import PartitionSpec as P

MESH = pl.DeviceIdType.MESH
LANES = 128
SUBLANES = 8
BLOCK = 2 * LANES
LAG = 2
VMEM_SPEC = pl.BlockSpec(memory_space=pltpu.VMEM)
ANY_SPEC = pl.BlockSpec(memory_space=pl.ANY)
F32 = jnp.float32
BF16 = jnp.bfloat16
HIGHEST = lax.Precision.HIGHEST
NN = ((1,), (0,))
NT = ((1,), (1,))


def split(x):
    high = x.astype(BF16)
    low = (x - high.astype(F32)).astype(BF16)
    return high, low


def dot(a, b, contract=NN):
    return lax.dot_general(a, b, (contract, ((), ())), preferred_element_type=F32)


class Layout:
    def __init__(self, rows, slab, core_axis):
        self.rows, self.slab, self.core_axis = rows, slab, core_axis
        self.n = rows * slab
        self.m = self.n // 2

    def split_index(self, r, s):
        if self.core_axis == "slab":
            return r * (self.slab // 2) + s // 2, s % 2
        return (r // 2) * self.slab + s, r % 2

    def place(self, q, c):
        if self.core_axis == "slab":
            half = self.slab // 2
            return q // half, 2 * (q % half) + c
        return 2 * (q // self.slab) + c, q % self.slab

    def of_device(self, d):
        return self.split_index(d // self.slab, d % self.slab)


def remote(src, dst, send, recv, where):
    return pltpu.make_async_remote_copy(
        src_ref=src, dst_ref=dst, send_sem=send, recv_sem=recv, device_id=where, device_id_type=MESH
    )


def pack(folded, share):
    groups = LANES // share
    rows = folded.shape[0] // groups
    if groups == 1:
        return folded
    return jnp.concatenate([folded[g * rows : (g + 1) * rows] for g in range(groups)], axis=1)


def unpack(chunk, share):
    groups = LANES // share
    if groups == 1:
        return chunk
    return jnp.concatenate([chunk[:, g * share : (g + 1) * share] for g in range(groups)], axis=0)


def kernel(lay, scale, snap_ref, start_ref, lin_ref, quad_ref, off_ref,
           proj_ref, red_ref, mis_ref,
           s_ref, cat_ref, yt_ref, pt_ref, quad_vmem, qcat_ref, work_ref, edge_ref, halo_ref, full_ref,
           part1, got1, mine1, recv1, part2, got2, mine2, recv2,
           load_sem, quad_sem, pair_send1, pair_recv1, far_send1, far_recv1,
           pair_send2, pair_recv2, far_send2, far_recv2,
           all_send, all_recv, fwd_send, fwd_recv, edge_send, edge_recv):
    n, m = lay.n, lay.m
    r, s = lax.axis_index("rows"), lax.axis_index("slab")
    me = r * lay.slab + s
    q, c = lay.split_index(r, s)
    partner = lay.place(q, 1 - c)
    rows, width = s_ref.shape
    rank = pt_ref.shape[0]
    share = width // n
    blocks = width // BLOCK
    qpb = m // blocks
    load = load_sem.shape[0]
    chunk = rows // load

    def fetch(b):
        at = pl.ds(b * chunk, chunk)
        return pltpu.make_async_copy(snap_ref.at[at], s_ref.at[at], load_sem.at[b])

    for b in range(load):
        fetch(b).start()
    quad_copy = pltpu.make_async_copy(quad_ref, quad_vmem, quad_sem)
    quad_copy.start()

    barrier = pltpu.get_barrier_semaphore()

    def greet(i, _):
        peer = (me + i) % n
        pl.semaphore_signal(barrier, inc=1, device_id=(peer // lay.slab, peer % lay.slab), device_id_type=MESH)
        return 0

    lax.fori_loop(1, n, greet, 0)

    def forward(b):
        both = dot(s_ref[b * chunk : (b + 1) * chunk, :], cat_ref[...])
        y = (both[:, :rank] + both[:, rank:]).T
        high, low = split(y)
        yt_ref[:rank, b * chunk : (b + 1) * chunk] = high
        yt_ref[rank:, b * chunk : (b + 1) * chunk] = low

    def each_other(fn):
        def one(i, _):
            fn((q + i) % m)
            return 0

        lax.fori_loop(1, m, one, 0)

    def scatter(part, got, mine, recv, pair_send, pair_recv, far_send, far_recv):
        def pair_copy(k):
            at = pl.ds(k * qpb, qpb)
            return remote(part.at[1 - c, at], got.at[at], pair_send.at[k], pair_recv.at[k], partner)

        def far_copy(target):
            return remote(mine.at[target], recv.at[q], far_send.at[target], far_recv.at[q], lay.place(target, c))

        def arrival(source):
            return remote(mine.at[source], recv.at[source], far_send.at[source], far_recv.at[source], lay.place(source, c))

        def relay(k):
            pair_copy(k).wait_recv()
            at = pl.ds(k * qpb, qpb)
            mine[at] = part[c, at] + got[at]
            for i in range(qpb):
                target = k * qpb + i

                @pl.when(target != q)
                def _():
                    far_copy(target).start()

        for k in range(blocks):
            both = dot(yt_ref[...], s_ref[:, k * BLOCK : (k + 1) * BLOCK])
            folded = both[:rank] + both[rank:]
            for i in range(BLOCK // share):
                dq, dc = lay.of_device(k * (BLOCK // share) + i)
                part[dc, dq] = pack(folded[:, i * share : (i + 1) * share], share)
            if k == 0 and part is part1:
                pl.semaphore_wait(barrier, n - 1)
            pair_copy(k).start()
            if k >= LAG:
                relay(k - LAG)
        for k in range(blocks - LAG, blocks):
            relay(k)

        def collect():
            def one(i, total):
                source = (q + i) % m
                arrival(source).wait_recv()
                return total + recv[source]

            return lax.fori_loop(1, m, one, mine[q])

        def drain():
            for k in range(blocks):
                pair_copy(k).wait_send()
            each_other(lambda target: far_copy(target).wait_send())

        return collect, drain

    cat_ref[...] = jnp.concatenate(split(start_ref[...].T), axis=1)
    for b in range(load):
        fetch(b).wait()
        forward(b)
    collect1, drain1 = scatter(part1, got1, mine1, recv1, pair_send1, pair_recv1, far_send1, far_recv1)
    full_ref[c, q] = collect1()

    def spread(target):
        return remote(full_ref.at[c, q], full_ref.at[c, q], all_send.at[target], all_recv.at[q], lay.place(target, c))

    def landed(source):
        return remote(
            full_ref.at[c, source], full_ref.at[c, source], all_send.at[source], all_recv.at[source], lay.place(source, c)
        )

    def across(source, half):
        return remote(
            full_ref.at[half, source], full_ref.at[half, source], fwd_send.at[source], fwd_recv.at[source], partner
        )

    each_other(lambda target: spread(target).start())
    across(q, c).start()

    def pass_on(source):
        landed(source).wait_recv()
        across(source, c).start()

    each_other(pass_on)
    across(q, 1 - c).wait_recv()
    each_other(lambda source: across(source, 1 - c).wait_recv())

    per = LANES // share
    for b in range(width // LANES):
        pieces = []
        for i in range(per):
            dq, dc = lay.of_device(b * per + i)
            pieces.append(unpack(full_ref[dc, dq], share))
        pt_ref[:, b * LANES : (b + 1) * LANES] = jnp.concatenate(pieces, axis=1) if per > 1 else pieces[0]
    cat_ref[...] = jnp.concatenate(split(pt_ref[...].T), axis=1)
    for b in range(load):
        forward(b)
    collect2, drain2 = scatter(part2, got2, mine2, recv2, pair_send2, pair_recv2, far_send2, far_recv2)

    phigh, plow = split(pt_ref[...])
    corr = dot(phigh, phigh, NT) + (dot(phigh, plow, NT) + dot(plow, phigh, NT))
    inverse = invert_factor(corr, work_ref)
    icat = jnp.concatenate(split(inverse), axis=0)
    ihigh = icat[:rank]
    for b in range(load):
        at = slice(b * chunk, (b + 1) * chunk)
        both = dot(icat, yt_ref[:rank, at])
        modes = both[:rank] + (both[rank:] + dot(ihigh, yt_ref[rank:, at]))
        proj_ref[:, at] = modes.astype(BF16)
    quad_copy.wait()
    qhigh, qlow = split(quad_vmem[...])
    qcat_ref[:rank, :] = qhigh
    qcat_ref[rank:, :] = qlow

    z = jnp.dot(inverse, unpack(collect2(), share), precision=HIGHEST, preferred_element_type=F32) * scale
    red_ref[...] = z
    edge_ref[...] = z.T[:SUBLANES]
    before = (me + n - 1) % n
    edge = remote(edge_ref, halo_ref, edge_send, edge_recv, (before // lay.slab, before % lay.slab))
    edge.start()

    state = z
    for _ in range(2):
        pairs = (state[:, None, :] * state[None, :, :]).reshape(rank * rank, share)
        pair_high, pair_low = split(pairs)
        both = dot(qcat_ref[...], pair_high)
        quad = both[:rank] + (both[rank:] + dot(qcat_ref[:rank, :], pair_low))
        change = jnp.dot(lin_ref[...], state, precision=HIGHEST, preferred_element_type=F32) + quad + off_ref[...]
        state = state + 0.25 * change
    edge.wait_recv()
    target = jnp.concatenate([z[:, 2:], halo_ref[...].T[:, :2]], axis=1)
    position = me * share + lax.broadcasted_iota(jnp.int32, (1, share), 1)
    mis_ref[...] = jnp.where(position < width - 2, state - target, 0.0)

    edge.wait_send()
    drain1()
    drain2()
    each_other(lambda other: spread(other).wait_send())
    across(q, c).wait_send()
    each_other(lambda other: across(other, c).wait_send())


def invert_factor(corr, work_ref):
    rank = corr.shape[0]
    row = lax.broadcasted_iota(jnp.int32, (rank, rank), 0)
    col = lax.broadcasted_iota(jnp.int32, (rank, rank), 1)
    eye = jnp.where(row == col, 1.0, 0.0).astype(F32)
    work_ref[...] = jnp.concatenate([corr, eye], axis=1)
    rows1 = lax.broadcasted_iota(jnp.int32, (rank, 1), 0)
    lanes = lax.broadcasted_iota(jnp.int32, (rank, 2 * rank), 1)
    lane1 = lax.broadcasted_iota(jnp.int32, (1, 2 * rank), 1)

    def eliminate(j, _):
        m = work_ref[...]
        pivot = work_ref[pl.ds(j, 1), :]
        column = jnp.sum(jnp.where(lanes == j, m, 0.0), axis=1, keepdims=True)
        d = jnp.sum(jnp.where(lane1 == j, pivot, 0.0), axis=1, keepdims=True)
        factor = jnp.where(rows1 > j, column / d, 0.0)
        work_ref[...] = m - factor * pivot
        return 0

    lax.fori_loop(0, rank, eliminate, 0)
    m = work_ref[...]
    diag = jnp.sum(jnp.where(row == col, m[:, :rank], 0.0), axis=1, keepdims=True)
    return m[:, rank:] / jnp.sqrt(diag)


def body(snapshots, start_block, linear_op, quad_op, offset, *, lay):
    rows, width = snapshots.shape
    rank = start_block.shape[1]
    n, m = lay.n, lay.m
    share = width // n
    tall = rank * share // LANES
    blocks = width // BLOCK
    load = 4
    scale = math.sqrt(width) / (rows * n)
    dma = lambda k: pltpu.SemaphoreType.DMA((k,))
    half = lambda: pltpu.VMEM((m, tall, LANES), F32)
    both = lambda: pltpu.VMEM((2, m, tall, LANES), F32)
    one = pltpu.SemaphoreType.DMA
    projection, reduced, mismatch = pl.pallas_call(
        functools.partial(kernel, lay, scale),
        in_specs=[ANY_SPEC, VMEM_SPEC, VMEM_SPEC, ANY_SPEC, VMEM_SPEC],
        out_specs=[VMEM_SPEC] * 3,
        out_shape=[
            jax.ShapeDtypeStruct((rank, rows), BF16),
            jax.ShapeDtypeStruct((rank, share), F32),
            jax.ShapeDtypeStruct((rank, share), F32),
        ],
        scratch_shapes=[
            pltpu.VMEM((rows, width), BF16),
            pltpu.VMEM((width, 2 * rank), BF16),
            pltpu.VMEM((2 * rank, rows), BF16),
            pltpu.VMEM((rank, width), F32),
            pltpu.VMEM((rank, rank * rank), F32),
            pltpu.VMEM((2 * rank, rank * rank), BF16),
            pltpu.VMEM((rank, 2 * rank), F32),
            pltpu.VMEM((SUBLANES, rank), F32),
            pltpu.VMEM((SUBLANES, rank), F32),
            both(),
            both(), half(), half(), half(),
            both(), half(), half(), half(),
            dma(load), one,
            dma(blocks), dma(blocks), dma(m), dma(m),
            dma(blocks), dma(blocks), dma(m), dma(m),
            dma(m), dma(m), dma(m), dma(m), one, one,
        ],
        compiler_params=pltpu.CompilerParams(collective_id=0, has_side_effects=True, vmem_limit_bytes=58 * 2**20),
        name="inference",
    )(snapshots, start_block.T, linear_op.T, quad_op.T, offset.reshape(rank, 1))
    return projection.T, reduced.T, mismatch.T


def solution(mesh):
    in_specs = (P(("rows", "slab"), None), P(), P(), P(), P())
    out_specs = (P(("rows", "slab"), None), P(("rows", "slab"), None), P(("rows", "slab"), None))
    grid = mesh.devices
    chip = lambda device: getattr(device, "coords", None)
    rows, slab = mesh.shape["rows"], mesh.shape["slab"]
    paired_rows = rows > 1 and chip(grid[0, 0]) is not None and chip(grid[0, 0]) == chip(grid[1, 0])
    lay = Layout(rows, slab, "rows" if paired_rows or slab % 2 else "slab")
    run = functools.partial(body, lay=lay)
    return jax.shard_map(run, mesh=mesh, in_specs=in_specs, out_specs=out_specs, check_vma=False)
```

time: 312 us -> 60.5 us (0.19)
  waiting for transfers between devices: 186 us -> 0 us
  Pallas kernels: 0 us -> 52.1 us
  matrix products: 46.9 us -> 0 us
  blocking collectives: 45.4 us -> 0 us
  between operations: 14.2 us -> 0.64 us
  other arithmetic: 13.3 us -> 0 us
  local copies, waits for them, and re-layouts: 3.4 us -> 7.39 us
    reduce_scatter x1 -> x0, waiting for transfers between devices: 185 us -> none  [body(): lax.psum_scatter(lax.dot_general(snapshots, snapshots, contract, preferre...]
    pallas_call x0 -> x1, Pallas kernels: none -> 52.1 us  [body(): pl.pallas_call(functools.partial(kernel, lay, scale), in_specs=[ANY_SPEC,...]
    dot_general x9 -> x0, matrix products: 45.7 us -> none  [the longest x1 24.4 us: body(): lax.dot_general(snapshots, snapshots, contract, preferred_element_type=jn...]
    all_gather x1 -> x0, blocking collectives: 45.4 us -> none  [body(): power = lax.all_gather(power_block, ('rows', 'slab'), axis=0, tiled=True)]
    another operation x5 -> x0, other arithmetic: 12.1 us -> none  [the longest x3 6.52 us: normalize(): factor = jnp.linalg.cholesky(jnp.dot(power.T, power, precision=highest))]
    unnamed x10 -> x4, local copies, waits for them, and re-layouts: 0.04 us -> 6.03 us
    mul x2 -> x0, local copies, waits for them, and re-layouts: 3.28 us -> none  [advance(): pairs = (state[:, :, None] * state[:, None, :]).reshape(state.shape[0], -1)]
  transfers between devices with their start and end apart: 2 -> 0, of which waited for: 2 -> 0; matrix products, arithmetic and copies ran while one was open for 1% -> 0% of each run, Pallas kernels for 0% -> 0%
where the time goes in v2:
time: 60.5 us; the launch traced here: 60.1 us
  Pallas kernels  52.1 us (86%)
  local copies, waits for them, and re-layouts  7.39 us (12%)
  between operations  0.64 us (1%)
    pallas_call x1, Pallas kernels, body(): pl.pallas_call(functools.partial(kernel, lay, scale), in_specs=[ANY_SPEC,...  52.1 us
    unnamed x4, local copies, waits for them, and re-layouts  6.03 us
    reshape x1, local copies, waits for them, and re-layouts, body(): offset.reshape(rank, 1)  1.36 us

profile of v2, /device:TPU:1, one launch (start us, length us, event | category | flops | bytes accessed | tf_op | source)
XLA Modules:
  0.0 60.1 jit_solution(17828982014047437359)
XLA Ops:
  0.6 1.5 %copy.8 = f32[64,64]{0,1:T(8,128)} copy(f32[64,64]{1,0:T(8,128)} %param.7) | data formatting | bytes 32768 | tf_op args[2]
  2.1 1.4 %copy.9.off_ref = f32[64,1]{1,0:T(8,128)} copy(f32[64,1]{0,1:T(1,128)} %bitcast.13) | data formatting | bytes 512 | tf_op jit(solution)/shard_map/reshape | solution.py:333
  3.4 52.1 %inference.1 = (bf16[64,2048]{1,0:T(8,128)(2,1)}, f32[64,64]{1,0:T(8,128)}, f32[64,64]{1,0:T(8,128)}) custom-call(bf16[2048,2048]{1,0:T(8,128)(2,1)} %snap_ref.1, f32[64,2048]{1,0:T(8,128)} %bitcast.8, f32[64,64]{1,0:T(8,128)} %bitcast.10, f32[64,4096]{1,0:T(8,128)} %bitcast.7, f32[64,1]{1,0:T(8,128)} %copy.9.off_ref), custom_call_target="tpu_custom_call" | custom-call | tf_op jit(solution)/shard_map/inference/pallas_call | solution.py:304
  55.5 1.5 %copy.10 = f32[64,64]{1,0:T(8,128)} copy(f32[64,64]{0,1:T(8,128)} %bitcast.12) | data formatting | bytes 32768
  57.0 1.5 %copy.11 = f32[64,64]{1,0:T(8,128)} copy(f32[64,64]{0,1:T(8,128)} %bitcast.11) | data formatting | bytes 32768
  58.4 1.7 %copy.13 = bf16[2048,64]{0,1:T(8,128)(2,1)} copy(bf16[2048,64]{0,1:T(8,128)(2,1)} %bitcast.9) | data formatting | bytes 524288

commit v3 on v2

--- a/solution.py
+++ b/solution.py
@@ -236,24 +236,26 @@
     qcat_ref[rank:, :] = qlow
 
     z = jnp.dot(inverse, unpack(collect2(), share), precision=HIGHEST, preferred_element_type=F32) * scale
-    red_ref[...] = z
-    edge_ref[...] = z.T[:SUBLANES]
+    reduced = z.T
+    red_ref[...] = reduced
+    edge_ref[...] = reduced[:SUBLANES]
     before = (me + n - 1) % n
     edge = remote(edge_ref, halo_ref, edge_send, edge_recv, (before // lay.slab, before % lay.slab))
     edge.start()
 
+    lin_t, off_t = lin_ref[...].T, off_ref[...].T
     state = z
     for _ in range(2):
         pairs = (state[:, None, :] * state[None, :, :]).reshape(rank * rank, share)
         pair_high, pair_low = split(pairs)
         both = dot(qcat_ref[...], pair_high)
         quad = both[:rank] + (both[rank:] + dot(qcat_ref[:rank, :], pair_low))
-        change = jnp.dot(lin_ref[...], state, precision=HIGHEST, preferred_element_type=F32) + quad + off_ref[...]
+        change = jnp.dot(lin_t, state, precision=HIGHEST, preferred_element_type=F32) + quad + off_t
         state = state + 0.25 * change
     edge.wait_recv()
     target = jnp.concatenate([z[:, 2:], halo_ref[...].T[:, :2]], axis=1)
     position = me * share + lax.broadcasted_iota(jnp.int32, (1, share), 1)
-    mis_ref[...] = jnp.where(position < width - 2, state - target, 0.0)
+    mis_ref[...] = jnp.where(position < width - 2, state - target, 0.0).T
 
     edge.wait_send()
     drain1()
@@ -261,6 +263,12 @@
     each_other(lambda other: spread(other).wait_send())
     across(q, c).wait_send()
     each_other(lambda other: across(other, c).wait_send())
+
+
+def emit_kernel(proj_in, red_in, mis_in, proj_ref, red_ref, mis_ref):
+    proj_ref[...] = proj_in[...]
+    red_ref[...] = red_in[...]
+    mis_ref[...] = mis_in[...]
 
 
 def invert_factor(corr, work_ref):
@@ -307,8 +315,8 @@
         out_specs=[VMEM_SPEC] * 3,
         out_shape=[
             jax.ShapeDtypeStruct((rank, rows), BF16),
-            jax.ShapeDtypeStruct((rank, share), F32),
-            jax.ShapeDtypeStruct((rank, share), F32),
+            jax.ShapeDtypeStruct((share, rank), F32),
+            jax.ShapeDtypeStruct((share, rank), F32),
         ],
         scratch_shapes=[
             pltpu.VMEM((rows, width), BF16),
@@ -330,8 +338,15 @@
         ],
         compiler_params=pltpu.CompilerParams(collective_id=0, has_side_effects=True, vmem_limit_bytes=58 * 2**20),
         name="inference",
-    )(snapshots, start_block.T, linear_op.T, quad_op.T, offset.reshape(rank, 1))
-    return projection.T, reduced.T, mismatch.T
+    )(snapshots, start_block.T, linear_op, quad_op.T, offset.reshape(1, rank))
+    projection, reduced, mismatch = pl.pallas_call(
+        emit_kernel,
+        in_specs=[VMEM_SPEC] * 3,
+        out_specs=[VMEM_SPEC] * 3,
+        out_shape=[jax.ShapeDtypeStruct(x.shape, x.dtype) for x in (projection, reduced, mismatch)],
+        name="emit",
+    )(projection, reduced, mismatch)
+    return projection.T, reduced, mismatch
 
 
 def solution(mesh):

time: 60.5 us -> 54.6 us (0.902)
  local copies, waits for them, and re-layouts: 7.39 us -> 0 us
  Pallas kernels: 52.1 us -> 53.8 us
    unnamed x4 -> x0, local copies, waits for them, and re-layouts: 6.03 us -> none
    pallas_call x0 -> x1, Pallas kernels: none -> 1.7 us  [body(): pl.pallas_call(emit_kernel, in_specs=[VMEM_SPEC] * 3, out_specs=[VMEM_SPE...]
    reshape x1 -> x0, local copies, waits for them, and re-layouts: 1.36 us -> none  [body(): offset.reshape(rank, 1)]
where the time goes in v3:
time: 54.6 us; the launch traced here: 54.5 us
  Pallas kernels  53.8 us (99%)
  between operations  0.64 us (1%)
    pallas_call x1, Pallas kernels, body(): pl.pallas_call(functools.partial(kernel, lay, scale), in_specs=[ANY_SPEC,...  52.1 us
    pallas_call x1, Pallas kernels, body(): pl.pallas_call(emit_kernel, in_specs=[VMEM_SPEC] * 3, out_specs=[VMEM_SPE...  1.7 us

profile of v3, /device:TPU:1, one launch (start us, length us, event | category | flops | bytes accessed | tf_op | source)
XLA Modules:
  0.0 54.5 jit_solution(2753034217425841249)
XLA Ops:
  0.6 52.1 %inference.1 = (bf16[64,2048]{1,0:T(8,128)(2,1)}, f32[64,64]{1,0:T(8,128)}, f32[64,64]{1,0:T(8,128)}) custom-call(bf16[2048,2048]{1,0:T(8,128)(2,1)} %snap_ref.1, f32[64,2048]{1,0:T(8,128)} %bitcast.5, f32[64,64]{1,0:T(8,128)} %lin_ref.1, f32[64,4096]{1,0:T(8,128)} %bitcast.4, f32[1,64]{1,0:T(1,128)} %bitcast.6), custom_call_target="tpu_custom_call" | custom-call | tf_op jit(solution)/shard_map/inference/pallas_call | solution.py:312
  52.8 1.7 %emit.1 = (bf16[64,2048]{1,0:T(8,128)(2,1)}, f32[64,64]{1,0:T(8,128)}, f32[64,64]{1,0:T(8,128)}) custom-call(bf16[64,2048]{1,0:T(8,128)(2,1)} %get-tuple-element.9.proj_in, f32[64,64]{1,0:T(8,128)} %get-tuple-element.10.red_in, f32[64,64]{1,0:T(8,128)} %get-tuple-element.11.mis_in), custom_call_target="tpu_custom_call" | custom-call | tf_op jit(solution)/shard_map/emit/pallas_call | solution.py:342
